TPU v7x, 32 devices: a whole 2x2x4 slice. The times are simulated.
32 devices in a mesh: dp: 4 (over x, core), expert: 8 (over z, y).
Axes of the slice: x: 2, y: 2, z: 4, core: 2. Of those that a mesh axis runs over, the one named last changes fastest.
Arguments:
- tokens: bfloat16 [32768, 768], P(('dp', 'expert')), may hold values from -6 to 6
- lengths: int32 [32, 4], P(('dp', 'expert')), may hold values from 1 to 512, 1024 in all within a row
- routes: int32 [32768, 2], P(('dp', 'expert')), may hold values from 0 to 9, all different within a row; in each aligned block of 1024 rows (0 to 1023, 1024 to 2047, ...) at most 307 rows name the same one
- gain_one: float32 [768], replicated, may hold values from 0.5 to 1.5
- w_query: bfloat16 [768, 768], replicated, may hold values from -0.21875 to 0.21875
- w_key: bfloat16 [768, 768], replicated, may hold values from -0.21875 to 0.21875
- w_value: bfloat16 [768, 768], replicated, may hold values from -0.21875 to 0.21875
- w_attn_out: bfloat16 [768, 768], replicated, may hold values from -0.875 to 0.875
- gain_two: float32 [768], replicated, may hold values from 0.5 to 1.5
- w_gate: float32 [768, 10], replicated, may hold values from -0.15625 to 0.15625
- frozen_in: bfloat16 [2, 3072, 768], replicated, may hold values from -0.21875 to 0.21875
- frozen_out: bfloat16 [2, 3072, 768], replicated, may hold values from -0.15625 to 0.15625
- new_in: bfloat16 [8, 3072, 768], P('expert', 'dp'), may hold values from -0.21875 to 0.21875
- new_out: bfloat16 [8, 3072, 768], P('expert', 'dp'), may hold values from -0.15625 to 0.15625
- out_grad: bfloat16 [32768, 768], P(('dp', 'expert')), may hold values from -6 to 6
Outputs:
- output: bfloat16 [32768, 768], P(('dp', 'expert'))
- x_grad: float32 [32768, 768], P(('dp', 'expert'))
- gain_one_grad: float32 [768], replicated
- w_query_grad: float32 [768, 768], replicated
- w_key_grad: float32 [768, 768], replicated
- w_value_grad: float32 [768, 768], replicated
- w_attn_out_grad: float32 [768, 768], replicated
- gain_two_grad: float32 [768], replicated
- w_gate_grad: float32 [768, 10], replicated
- new_in_grad: float32 [8, 3072, 768], P('expert', 'dp')
- new_out_grad: float32 [8, 3072, 768], P('expert', 'dp')
Inputs may be any that keep to these rules, and one draw needn't show every extreme that they name: `routes`: each row names two different experts; among the 1024 rows of one sequence no expert is named more than 307 times, a bound that some block reaches; every expert is named somewhere. Each row holds the lengths of 4 documents in order; they sum to 1024, the longest is exactly 512.
All inputs are finite; a program needn't handle non-finite values.
Results may differ from a plain program's by a relative error of at most 0.013.
Values may be sent and summed in bfloat16 or wider, within the bound.
A program may use at most 320 MiB of HBM per device.

v0:
```python
import jax
import jax.numpy as jnp
from jax import lax
from jax.sharding import PartitionSpec as P

HEADS = 12


highest = lax.Precision.HIGHEST
epsilon = 1e-05
masked_score = -1000000000.0


def norm_forward(inputs, gain):
    centre = inputs - jnp.mean(inputs, axis=-1, keepdims=True)
    scale_inv = lax.rsqrt(jnp.mean(centre * centre, axis=-1, keepdims=True) + epsilon)
    normal_part = centre * scale_inv
    return (normal_part * gain, normal_part, scale_inv)


def norm_backward(upstream, gain, normal_part, scale_inv):
    scaled = upstream * gain
    inner = (
        scaled
        - jnp.mean(scaled, axis=-1, keepdims=True)
        - normal_part * jnp.mean(scaled * normal_part, axis=-1, keepdims=True)
    )
    return (inner * scale_inv, jnp.sum(upstream * normal_part, axis=0))


def doc_ids(length_row, seq_len):
    ends = jnp.cumsum(length_row)
    places = jnp.arange(seq_len, dtype=jnp.int32)
    return jnp.sum((places[:, None] >= ends[None, :]).astype(jnp.int32), axis=1)


def slot_tables(route_row, experts, capacity, seq_len):
    flat = route_row.reshape(-1)
    picks = (flat[:, None] == jnp.arange(experts, dtype=jnp.int32)[None, :]).astype(jnp.int32)
    ranks = jnp.sum((jnp.cumsum(picks, axis=0) - 1) * picks, axis=1)
    spots = flat * capacity + ranks
    owners = jnp.full((experts * capacity,), 2 * seq_len, jnp.int32)
    owners = owners.at[spots].set(jnp.arange(2 * seq_len, dtype=jnp.int32))
    return (spots, owners)


def block_scores(query_part, keys, doc_part, place_part, doc, places, scale):
    scores = (
        jnp.einsum("qhd,khd->hqk", query_part, keys, preferred_element_type=jnp.float32) * scale
    )
    allowed = (doc_part[:, None] == doc[None, :]) & (places[None, :] <= place_part[:, None])
    return jnp.where(allowed[None], scores, masked_score)


def gelu_grad(pre, upstream):
    return jax.vjp(jax.nn.gelu, pre)[1](upstream)[0]


def expert_forward(rows, w_in_full, w_out_full):
    pre = jnp.einsum("rd,fd->rf", rows, w_in_full, preferred_element_type=jnp.float32)
    act = jax.nn.gelu(pre).astype(jnp.bfloat16)
    return (jnp.dot(act, w_out_full, preferred_element_type=jnp.float32).astype(jnp.bfloat16), pre)


def expert_backward(grads, pre, w_in_full, w_out_full):
    act_grad = jnp.einsum("rd,fd->rf", grads, w_out_full, preferred_element_type=jnp.float32)
    pre_grad = gelu_grad(pre, act_grad).astype(jnp.bfloat16)
    return (
        jnp.dot(pre_grad, w_in_full, preferred_element_type=jnp.float32).astype(jnp.bfloat16),
        pre_grad,
    )


def on_device(
    tokens,
    lengths,
    routes,
    gain_one,
    w_query,
    w_key,
    w_value,
    w_attn_out,
    gain_two,
    w_gate,
    frozen_in,
    frozen_out,
    new_in,
    new_out,
    out_grad,
):
    seq_len, width = tokens.shape
    head_dim = width // HEADS
    scale = head_dim ** (-0.5)
    experts = w_gate.shape[1]
    frozen = frozen_in.shape[0]
    capacity = max(2, 3 * seq_len // experts)
    block = min(512, seq_len)
    blocks = seq_len // block
    split_shape = (seq_len, HEADS, head_dim)
    x_in = tokens.astype(jnp.float32)
    norm_one, normal_one, inv_one = norm_forward(x_in, gain_one)
    normed = norm_one.astype(jnp.bfloat16)
    query = (
        jnp.dot(normed, w_query, preferred_element_type=jnp.float32)
        .astype(jnp.bfloat16)
        .reshape(split_shape)
    )
    keys = (
        jnp.dot(normed, w_key, preferred_element_type=jnp.float32)
        .astype(jnp.bfloat16)
        .reshape(split_shape)
    )
    values = (
        jnp.dot(normed, w_value, preferred_element_type=jnp.float32)
        .astype(jnp.bfloat16)
        .reshape(split_shape)
    )
    doc = doc_ids(lengths[0], seq_len)
    places = jnp.arange(seq_len, dtype=jnp.int32)

    def attend_block(index):
        start = index * block
        query_part = lax.dynamic_slice_in_dim(query, start, block, 0)
        scores = block_scores(
            query_part,
            keys,
            lax.dynamic_slice_in_dim(doc, start, block, 0),
            lax.dynamic_slice_in_dim(places, start, block, 0),
            doc,
            places,
            scale,
        )
        top = jnp.max(scores, axis=-1, keepdims=True)
        expd = jnp.exp(scores - top)
        total = jnp.sum(expd, axis=-1, keepdims=True)
        probs = (expd / total).astype(jnp.bfloat16)
        mixed_part = jnp.einsum("hqk,khd->qhd", probs, values, preferred_element_type=jnp.float32)
        return (mixed_part, (top + jnp.log(total))[..., 0])

    mixed_parts, log_totals = lax.map(attend_block, jnp.arange(blocks))
    mixed = mixed_parts.reshape(seq_len, width).astype(jnp.bfloat16)
    hidden = x_in + jnp.dot(mixed, w_attn_out, preferred_element_type=jnp.float32)
    norm_two, normal_two, inv_two = norm_forward(hidden, gain_two)
    logits = jnp.dot(norm_two, w_gate, precision=highest)
    picks = (routes[:, :, None] == jnp.arange(experts, dtype=jnp.int32)[None, None, :]).astype(
        jnp.float32
    )
    chosen = jnp.einsum("te,tke->tk", logits, picks, precision=highest)
    weights = jnp.exp(chosen - jnp.max(chosen, axis=1, keepdims=True))
    gates = weights / jnp.sum(weights, axis=1, keepdims=True)
    spots, owners = slot_tables(routes, experts, capacity, seq_len)
    zero_row = jnp.zeros((1, width), jnp.bfloat16)
    rows = jnp.concatenate([norm_two.astype(jnp.bfloat16), zero_row], axis=0)[owners // 2].reshape(
        experts, capacity, width
    )
    out_cot = out_grad.astype(jnp.float32)
    choice_grads = (
        (gates[:, :, None] * out_cot[:, None, :]).astype(jnp.bfloat16).reshape(2 * seq_len, width)
    )
    slot_grads = jnp.concatenate([choice_grads, zero_row], axis=0)[owners].reshape(
        experts, capacity, width
    )
    frozen_outputs = []
    frozen_back = []
    for expert in range(frozen):
        produced, pre = expert_forward(rows[expert], frozen_in[expert], frozen_out[expert])
        returned_rows, unused_grad = expert_backward(
            slot_grads[expert], pre, frozen_in[expert], frozen_out[expert]
        )
        frozen_outputs.append(produced)
        frozen_back.append(returned_rows)
    send_rows = rows[frozen:]
    send_grads = slot_grads[frozen:]
    arrived = lax.all_to_all(send_rows, "expert", split_axis=0, concat_axis=0, tiled=True)
    flat_rows = arrived.reshape(-1, width)
    used_rows = flat_rows
    hidden_units = new_in.shape[1] * lax.axis_size("dp")
    initial = (
        jnp.zeros((flat_rows.shape[0], width), jnp.float32),
        jnp.zeros((flat_rows.shape[0], hidden_units), jnp.float32),
    )
    pieces = (
        lax.all_gather(new_in, "dp", axis=1, tiled=True),
        lax.all_gather(new_out, "dp", axis=1, tiled=True),
    )
    total, pre_all = initial
    pre_part = jnp.einsum("rd,fd->rf", flat_rows, pieces[0][0], preferred_element_type=jnp.float32)
    act_part = jax.nn.gelu(pre_part).astype(jnp.bfloat16)
    total = jnp.dot(act_part, pieces[1][0], preferred_element_type=jnp.float32)
    total, pre = (total, pre_part)
    produced = total.astype(jnp.bfloat16)
    outputs = produced.reshape(arrived.shape)
    returned = lax.all_to_all(outputs, "expert", split_axis=0, concat_axis=0, tiled=True)
    arrived_grads = lax.all_to_all(send_grads, "expert", split_axis=0, concat_axis=0, tiled=True)
    pre, used_rows = (pre, used_rows)
    flat_grads = arrived_grads.reshape(-1, width)
    initial = (
        jnp.zeros((flat_grads.shape[0], width), jnp.float32),
        jnp.zeros(pre.shape, jnp.bfloat16),
    )
    pieces = (
        lax.all_gather(new_in, "dp", axis=1, tiled=True),
        lax.all_gather(new_out, "dp", axis=1, tiled=True),
    )
    total, grad_all = initial
    pre_part = pre
    act_grad = jnp.einsum("rd,fd->rf", flat_grads, pieces[1][0], preferred_element_type=jnp.float32)
    part_grad = gelu_grad(pre_part, act_grad).astype(jnp.bfloat16)
    total = jnp.dot(part_grad, pieces[0][0], preferred_element_type=jnp.float32)
    total, pre_grad = (total, part_grad)
    rows_back = total.astype(jnp.bfloat16)
    act = jax.nn.gelu(pre).astype(jnp.bfloat16)
    w_in_grad = jnp.einsum("rf,rd->fd", pre_grad, used_rows, preferred_element_type=jnp.float32)
    w_out_grad = jnp.einsum("rf,rd->fd", act, flat_grads, preferred_element_type=jnp.float32)
    rows_back, w_in_grad, w_out_grad = (rows_back.reshape(arrived.shape), w_in_grad, w_out_grad)
    returned_grads = lax.all_to_all(rows_back, "expert", split_axis=0, concat_axis=0, tiled=True)
    all_outputs = jnp.concatenate([jnp.stack(frozen_outputs), returned], axis=0).reshape(
        experts * capacity, width
    )
    picked = all_outputs[spots].astype(jnp.float32).reshape(seq_len, 2, width)
    output = (hidden + jnp.sum(gates[:, :, None] * picked, axis=1)).astype(jnp.bfloat16)
    all_back = jnp.concatenate([jnp.stack(frozen_back), returned_grads], axis=0).reshape(
        experts * capacity, width
    )
    back_rows = all_back[spots].astype(jnp.float32).reshape(seq_len, 2, width)
    gate_terms = jnp.sum(out_cot[:, None, :] * picked, axis=2)
    logit_grads = gates * (gate_terms - jnp.sum(gates * gate_terms, axis=1, keepdims=True))
    full_logit_grad = jnp.einsum("tk,tke->te", logit_grads, picks, precision=highest)
    w_gate_grad = jnp.dot(norm_two.T, full_logit_grad, precision=highest)
    normed_two_grad = jnp.sum(back_rows, axis=1) + jnp.dot(
        full_logit_grad, w_gate.T, precision=highest
    )
    hidden_part, gain_two_grad = norm_backward(normed_two_grad, gain_two, normal_two, inv_two)
    hidden_grad = out_cot + hidden_part
    branch_grad = hidden_grad.astype(jnp.bfloat16)
    w_attn_out_grad = jnp.einsum(
        "td,te->de", mixed, branch_grad, preferred_element_type=jnp.float32
    )
    mixed_grad = (
        jnp.einsum("te,de->td", branch_grad, w_attn_out, preferred_element_type=jnp.float32)
        .astype(jnp.bfloat16)
        .reshape(split_shape)
    )

    def attend_back(carry, index):
        key_acc, value_acc = carry
        start = index * block
        query_part = lax.dynamic_slice_in_dim(query, start, block, 0)
        grad_part = lax.dynamic_slice_in_dim(mixed_grad, start, block, 0)
        scores = block_scores(
            query_part,
            keys,
            lax.dynamic_slice_in_dim(doc, start, block, 0),
            lax.dynamic_slice_in_dim(places, start, block, 0),
            doc,
            places,
            scale,
        )
        probs = jnp.exp(scores - log_totals[index][:, :, None])
        prob_grad = jnp.einsum(
            "qhd,khd->hqk", grad_part, values, preferred_element_type=jnp.float32
        )
        delta = jnp.sum(probs * prob_grad, axis=-1, keepdims=True)
        score_grad = (probs * (prob_grad - delta)).astype(jnp.bfloat16)
        query_grad = (
            jnp.einsum("hqk,khd->qhd", score_grad, keys, preferred_element_type=jnp.float32) * scale
        )
        key_acc = (
            key_acc
            + jnp.einsum("hqk,qhd->khd", score_grad, query_part, preferred_element_type=jnp.float32)
            * scale
        )
        value_acc = value_acc + jnp.einsum(
            "hqk,qhd->khd",
            probs.astype(jnp.bfloat16),
            grad_part,
            preferred_element_type=jnp.float32,
        )
        return ((key_acc, value_acc), query_grad.astype(jnp.bfloat16))

    zero_heads = jnp.zeros(split_shape, jnp.float32)
    (key_sum, value_sum), query_blocks = lax.scan(
        attend_back, (zero_heads, zero_heads), jnp.arange(blocks)
    )
    query_grad = query_blocks.reshape(seq_len, width)
    key_grad = key_sum.astype(jnp.bfloat16).reshape(seq_len, width)
    value_grad = value_sum.astype(jnp.bfloat16).reshape(seq_len, width)
    w_query_grad = jnp.einsum("td,te->de", normed, query_grad, preferred_element_type=jnp.float32)
    w_key_grad = jnp.einsum("td,te->de", normed, key_grad, preferred_element_type=jnp.float32)
    w_value_grad = jnp.einsum("td,te->de", normed, value_grad, preferred_element_type=jnp.float32)
    normed_grad = jnp.einsum("te,de->td", query_grad, w_query, preferred_element_type=jnp.float32)
    normed_grad = normed_grad + jnp.einsum(
        "te,de->td", key_grad, w_key, preferred_element_type=jnp.float32
    )
    normed_grad = normed_grad + jnp.einsum(
        "te,de->td", value_grad, w_value, preferred_element_type=jnp.float32
    )
    input_part, gain_one_grad = norm_backward(normed_grad, gain_one, normal_one, inv_one)
    x_grad = hidden_grad + input_part
    new_in_grad, new_out_grad = (
        lax.psum_scatter(w_in_grad[None], "dp", scatter_dimension=1, tiled=True),
        lax.psum_scatter(w_out_grad[None], "dp", scatter_dimension=1, tiled=True),
    )
    shared = lax.psum(
        (
            gain_one_grad,
            w_query_grad,
            w_key_grad,
            w_value_grad,
            w_attn_out_grad,
            gain_two_grad,
            w_gate_grad,
        ),
        ("dp", "expert"),
    )
    return (
        output,
        x_grad,
        shared[0],
        shared[1],
        shared[2],
        shared[3],
        shared[4],
        shared[5],
        shared[6],
        new_in_grad,
        new_out_grad,
    )


def solution(mesh):
    return jax.shard_map(
        on_device,
        mesh=mesh,
        in_specs=(
            P(("dp", "expert"), None),
            P(("dp", "expert"), None),
            P(("dp", "expert"), None),
            P(),
            P(),
            P(),
            P(),
            P(),
            P(),
            P(),
            P(),
            P(),
            P("expert", "dp", None),
            P("expert", "dp", None),
            P(("dp", "expert"), None),
        ),
        out_specs=(
            P(("dp", "expert"), None),
            P(("dp", "expert"), None),
            P(),
            P(),
            P(),
            P(),
            P(),
            P(),
            P(),
            P("expert", "dp", None),
            P("expert", "dp", None),
        ),
        check_vma=False,
    )
```

profile of v0, /device:TPU:0, one launch (start us, length us, event | category | flops | bytes accessed | tf_op | source)
XLA Modules:
  0.0 1183.8 jit_solution(7240857974431699052)
XLA Ops:
  35.2 76.0 %while.29 = (s32[]{:T(128)}, bf16[2,512,12,64]{1,3,2,0:T(8,128)(2,1)}, f32[2,12,512]{2,1,0:T(8,128)S(1)}, s32[2]{0:T(128)S(1)}, s32[1024]{0:T(1024)S(1)}, /*inde...) while((s32[]{:T(128)}, ...), condition=%wide.region_7.8_spmd.clone, body=%wide.region_4.7_spmd.clone.sunk | while | flops 1687676928 | bytes 190296336 | solution.py:140
  118.7 14.0 %gather_fusion = bf16[3070,768]{1,0:T(8,128)(2,1)} fusion(bf16[1025,768]{1,0:T(8,128)(2,1)S(1)} %concatenate.12, s32[3072]{0:T(1024)S(1)} %get-tuple-element.293), kind=kCustom, calls=%fused_computation | custom fusion | bytes 9443320 | tf_op jit(solution)/shard_map/gather | solution.py:153
  182.9 16.8 %gather_fusion.2 = bf16[3070,768]{1,0:T(8,128)(2,1)} fusion(bf16[2049,768]{1,0:T(8,128)(2,1)} %concatenate.14, s32[3072]{0:T(1024)S(1)} %get-tuple-element.292), kind=kCustom, calls=%fused_computation.2 | custom fusion | bytes 9443320 | tf_op jit(solution)/shard_map/gather | solution.py:160
  209.7 25.9 %all-to-all-done = bf16[8,307,768]{2,1,0:T(8,128)(2,1)} async-done(((bf16[8,307,768]{2,1,0:T(8,128)(2,1)}), bf16[8,307,768]{2,1,0:T(8,128)(2,1)}, u32[]{:S(2)}, u32[]{:S(2)}) %all-to-all-start) | async-done | bytes 3772448 | tf_op jit(solution)/shard_map/all_to_all | solution.py:174
  258.3 66.6 %all-to-all-done.2 = bf16[8,307,768]{2,1,0:T(8,128)(2,1)} async-done(((bf16[8,307,768]{2,1,0:T(8,128)(2,1)}), bf16[8,307,768]{2,1,0:T(8,128)(2,1)}, u32[]{:S(2)}, u32[]{:S(2)}) %all-to-all-start.2) | async-done | bytes 3772448 | tf_op jit(solution)/shard_map/all_to_all | solution.py:194
  330.1 20.3 %fusion.38 = f32[2456,3072]{1,0:T(8,128)} fusion(bf16[2456,768]{1,0:T(8,128)(2,1)} %reshape.359, bf16[1,3072,768]{2,1,0:T(8,128)(2,1)} %all-gather.3.cloned.1.call-done), kind=kOutput, calls=%fused_computation.73 | convolution fusion | flops 11588861952 | bytes 38670336 | tf_op jit(solution)/shard_map/rd,fd->rf/dot_general | solution.py:187
  350.3 24.1 %convolution_convert_fusion.1 = bf16[2456,768]{1,0:T(8,128)(2,1)} fusion(bf16[1,3072,768]{2,1,0:T(8,128)(2,1)} %all-gather.5.cloned.1.call-done, f32[2456,3072]{1,0:T(8,128)} %fusion.38), kind=kOutput, calls=%fused_computation.64 | convolution fusion | flops 11658651648 | bytes 38670336 | tf_op jit(solution)/shard_map/dot_general | solution.py:189
  384.4 37.1 %fusion.34 = bf16[2456,3072]{1,0:T(8,128)(2,1)} fusion(f32[2456,3072]{1,0:T(8,128)} %fusion.38, bf16[2456,768]{1,0:T(8,128)(2,1)} %reshape.362, bf16[1,3072,768]{2,1,0:T(8,128)(2,1)} %all-gather.5.cloned.1.call-done), kind=kOutput, calls=%fused_computation.52 | convolution fusion | flops 11739758592 | bytes 53760000 | tf_op jit(solution)/shard_map/rd,fd->rf/dot_general | solution.py:207
  421.4 17.9 %convolution_convert_fusion = bf16[2456,768]{1,0:T(8,128)(2,1)} fusion(bf16[2456,3072]{1,0:T(8,128)(2,1)} %fusion.34, bf16[1,3072,768]{2,1,0:T(8,128)(2,1)} %all-gather.3.cloned.1.call-done), kind=kOutput, calls=%fused_computation.63 | convolution fusion | flops 11590748160 | bytes 23580672 | tf_op jit(solution)/shard_map/dot_general | solution.py:209
  444.3 24.9 %all-to-all-done.1 = bf16[8,307,768]{2,1,0:T(8,128)(2,1)} async-done(((bf16[8,307,768]{2,1,0:T(8,128)(2,1)}), bf16[8,307,768]{2,1,0:T(8,128)(2,1)}, u32[]{:S(2)}, u32[]{:S(2)}) %all-to-all-start.1) | async-done | bytes 3772448 | tf_op jit(solution)/shard_map/all_to_all | solution.py:193
  539.1 17.2 %multiply_reduce_fusion.1 = (f32[1024,2]{1,0:T(8,128)S(1)}, f32[1024,768]{1,0:T(8,128)}) fusion(f32[1024,2,768]{2,1,0:T(2,128)} %reshape.369, f32[1024,768]{1,0:T(8,128)} %convert_element_type.144, f32[1024,2]{1,0:T(8,128)S(1)} %copy-done.24), kind=kLoop, calls=%fused_computation.54 | loop fusion | flops 5502976 | bytes 12599296 | tf_op jit(solution)/shard_map/reduce_sum | solution.py:226
  620.7 174.7 %while.30 = (s32[]{:T(128)}, f32[1024,12,64]{0,2,1:T(8,128)}, f32[1024,12,64]{0,2,1:T(8,128)}, bf16[2,512,12,64]{1,3,2,0:T(8,128)(2,1)}, s32[2]{0:T(128)S(1)}, /...) while((s32[]{:T(128)}, f32[1024,12,64]{0,2,1:T(8,128)}, ...), condition=%wide.region_24.25_spmd.clone.clone, body=%wide.region_22.24_spmd.clone.clone.sunk | while | flops 4127188992 | bytes 218566960 | solution.py:282
  636.3 13.4 %bitcast_add_fusion.5 = f32[1024,12,64]{0,2,1:T(8,128)} fusion(f32[1024,12,64]{0,2,1:T(8,128)} %get-tuple-element.488, f32[12,512,1024]{2,1,0:T(8,128)} %fusion.253, f32[12,512]{1,0:T(8,128)S(1)} %dynamic-slice_bitcast_fusion.2, pred[512,1024]{1,0:T(8,128)(4,1)S(1)} %compare_and_fusion.5, pred[]{:T(512)S(6)} %compare.7, ...), kind=kOutput, calls=%fused_computation.25.clone.1 | convolution fusion | flops 832045056 | bytes 32800772 | tf_op jit(solution)/shard_map/while/body/eval_jaxpr/hqk,qhd->khd/dot_general | solution.py:273
  649.7 18.1 %multiply_reduce_fusion.10 = (f32[12,512]{1,0:T(8,128)S(1)}, f32[12,512,1024]{2,1,0:T(8,128)}) fusion(f32[12,512,1024]{2,1,0:T(8,128)} %fusion.253, f32[12,512]{1,0:T(8,128)S(1)} %dynamic-slice_bitcast_fusion.2, pred[512,1024]{1,0:T(8,128)(4,1)S(1)} %compare_and_fusion.5, bf16[1024,12,64]{0,2,1:T(8,128)(2,1)} %get-tuple-element.514, ...), kind=kOutput, calls=%fused_computation.20.clone.1 | convolution fusion | flops 836757504 | bytes 53264388 | tf_op jit(solution)/shard_map/while/body/eval_jaxpr/qhd,khd->hqk/dot_general | solution.py:260
  667.8 21.2 %multiply_convert_fusion.20 = bf16[12,512,1024]{2,1,0:T(8,128)(2,1)} fusion(f32[12,512,1024]{2,1,0:T(8,128)} %get-tuple-element.428, f32[12,512,1024]{2,1,0:T(8,128)} %fusion.253, f32[12,512]{1,0:T(8,128)S(1)} %get-tuple-element.429, f32[12,512]{1,0:T(8,128)S(1)} %dynamic-slice_bitcast_fusion.2, pred[512,1024]{1,0:T(8,128)(4,1)S(1)} %compare_and_fusion.5), kind=kLoop, calls=%fused_computation.19.clone.1 | loop fusion | flops 37748736 | bytes 63488000 | tf_op jit(solution)/shard_map/while/body/eval_jaxpr/convert_element_type | solution.py:264
  722.4 14.4 %bitcast_add_fusion.5 = f32[1024,12,64]{0,2,1:T(8,128)} fusion(f32[1024,12,64]{0,2,1:T(8,128)} %get-tuple-element.488, f32[12,512,1024]{2,1,0:T(8,128)} %fusion.253, f32[12,512]{1,0:T(8,128)S(1)} %dynamic-slice_bitcast_fusion.2, pred[512,1024]{1,0:T(8,128)(4,1)S(1)} %compare_and_fusion.5, pred[]{:T(512)S(6)} %compare.7, ...), kind=kOutput, calls=%fused_computation.25.clone.1 | convolution fusion | flops 832045056 | bytes 32800772 | tf_op jit(solution)/shard_map/while/body/eval_jaxpr/hqk,qhd->khd/dot_general | solution.py:273
  736.8 18.1 %multiply_reduce_fusion.10 = (f32[12,512]{1,0:T(8,128)S(1)}, f32[12,512,1024]{2,1,0:T(8,128)}) fusion(f32[12,512,1024]{2,1,0:T(8,128)} %fusion.253, f32[12,512]{1,0:T(8,128)S(1)} %dynamic-slice_bitcast_fusion.2, pred[512,1024]{1,0:T(8,128)(4,1)S(1)} %compare_and_fusion.5, bf16[1024,12,64]{0,2,1:T(8,128)(2,1)} %get-tuple-element.514, ...), kind=kOutput, calls=%fused_computation.20.clone.1 | convolution fusion | flops 836757504 | bytes 53264388 | tf_op jit(solution)/shard_map/while/body/eval_jaxpr/qhd,khd->hqk/dot_general | solution.py:260
  755.0 21.2 %multiply_convert_fusion.20 = bf16[12,512,1024]{2,1,0:T(8,128)(2,1)} fusion(f32[12,512,1024]{2,1,0:T(8,128)} %get-tuple-element.428, f32[12,512,1024]{2,1,0:T(8,128)} %fusion.253, f32[12,512]{1,0:T(8,128)S(1)} %get-tuple-element.429, f32[12,512]{1,0:T(8,128)S(1)} %dynamic-slice_bitcast_fusion.2, pred[512,1024]{1,0:T(8,128)(4,1)S(1)} %compare_and_fusion.5), kind=kLoop, calls=%fused_computation.19.clone.1 | loop fusion | flops 37748736 | bytes 63488000 | tf_op jit(solution)/shard_map/while/body/eval_jaxpr/convert_element_type | solution.py:264
  812.3 17.8 %convolution_bitcast_fusion.1 = f32[1,3072,768]{2,1,0:T(8,128)} fusion(bf16[2456,3072]{1,0:T(8,128)(2,1)} %fusion.34, bf16[2456,768]{1,0:T(8,128)(2,1)} %reshape.359), kind=kOutput, calls=%fused_computation.58 | convolution fusion | flops 11588861952 | bytes 28299264 | tf_op jit(solution)/shard_map/rf,rd->fd/dot_general | solution.py:213
  830.2 22.5 %convolution_bitcast_fusion = f32[1,3072,768]{2,1,0:T(8,128)} fusion(bf16[2456,768]{1,0:T(8,128)(2,1)} %reshape.362, f32[2456,3072]{1,0:T(8,128)} %fusion.38), kind=kOutput, calls=%fused_computation.57 | convolution fusion | flops 11656765440 | bytes 43388928 | tf_op jit(solution)/shard_map/rf,rd->fd/dot_general | solution.py:214
  865.4 42.0 %all-reduce.2 = (f32[768]{0:T(1024)}, f32[768]{0:T(1024)}, f32[768,10]{0,1:T(8,128)}) all-reduce(f32[768]{0:T(1024)S(1)} %get-tuple-element.227, f32[768]{0:T(1024)S(1)} %copy-done.65, f32[768,10]{0,1:T(8,128)S(1)} %fusion.91), channel_id=1, replica_groups=mesh['dp'=4,'expert'=8] {'dp','expert'}, use_global_device_ids=true, to_apply=%region_28.29 | all-reduce | flops 9216 | bytes 73728 | tf_op jit(solution)/shard_map/psum | solution.py:304
  912.0 93.3 %all-reduce.6.cloned.1.call-done = (f32[768,768]{1,0:T(8,128)}, f32[768,768]{1,0:T(8,128)}, f32[768,768]{1,0:T(8,128)}, f32[768,768]{1,0:T(8,128)}) async-done(((f32[768,768]{1,0:T(8,128)}, f32[768,768]{1,0:T(8,128)}, f32[768,768]{1,0:T(8,128)}, f32[768,768]{1,0:T(8,128)}), (f32[768,768]{1,0:T(8,128)}, f32[768,768]{1,0:T(8,128)}, f32[768,768]{1,0:T(8,128)}, ...) | async-done | bytes 9437200 | tf_op jit(solution)/shard_map/psum | solution.py:304
  1005.4 81.0 %reduce-scatter.3.cloned.1.call-done = f32[1,768,768]{2,1,0:T(8,128)} async-done(((f32[1,3072,768]{2,1,0:T(8,128)}), f32[1,768,768]{2,1,0:T(8,128)}) %reduce-scatter.3.cloned.1.call-update) | async-done | bytes 2359312 | tf_op jit(solution)/shard_map/reduce_scatter | solution.py:301
  1086.4 81.0 %reduce-scatter.5.cloned.1.call-done = f32[1,768,768]{2,1,0:T(8,128)} async-done(((f32[1,3072,768]{2,1,0:T(8,128)}), f32[1,768,768]{2,1,0:T(8,128)}) %reduce-scatter.5.cloned.1.call-update) | async-done | bytes 2359312 | tf_op jit(solution)/shard_map/reduce_scatter | solution.py:302
  (308 shorter events, 452.6 us)
Async XLA Ops:
  7.2 20.3 %copy-start = (bf16[768,768]{1,0:T(8,128)(2,1)S(1)}, bf16[768,768]{1,0:T(8,128)(2,1)}, u32[]{:S(2)}) copy-start(bf16[768,768]{1,0:T(8,128)(2,1)} %param.25) | copy-start | bytes 3538948
  9.3 18.2 %copy-start.63 = (f32[768]{0:T(1024)S(1)}, f32[768]{0:T(1024)}, u32[]{:S(2)}) copy-start(f32[768]{0:T(1024)} %param.22) | copy-start | bytes 9220
  12.2 20.0 %copy-start.53 = (f32[1024]{0:T(1024)}, f32[1024]{0:T(1024)S(1)}, u32[]{:S(2)}) copy-start(f32[1024]{0:T(1024)S(1)} %broadcast_multiply_fusion.6) | copy-start | bytes 12292
  12.8 19.4 %copy-start.59 = (f32[1024]{0:T(1024)}, f32[1024]{0:T(1024)S(1)}, u32[]{:S(2)}) copy-start(f32[1024]{0:T(1024)S(1)} %add_rsqrt_fusion.1) | copy-start | bytes 12292
  37.2 24.4 %copy-start.7 = (bf16[1024,12,64]{0,2,1:T(8,128)(2,1)S(1)}, bf16[1024,12,64]{0,2,1:T(8,128)(2,1)}, u32[]{:S(2)}) copy-start(bf16[1024,12,64]{0,2,1:T(8,128)(2,1)} %get-tuple-element.464) | copy-start | bytes 4718596 | tf_op jit(solution)/shard_map/while
  75.1 24.4 %copy-start.7 = (bf16[1024,12,64]{0,2,1:T(8,128)(2,1)S(1)}, bf16[1024,12,64]{0,2,1:T(8,128)(2,1)}, u32[]{:S(2)}) copy-start(bf16[1024,12,64]{0,2,1:T(8,128)(2,1)} %get-tuple-element.464) | copy-start | bytes 4718596 | tf_op jit(solution)/shard_map/while
  117.0 33.7 %copy-start.40 = (f32[1024]{0:T(1024)}, f32[1024]{0:T(1024)S(1)}, u32[]{:S(2)}) copy-start(f32[1024]{0:T(1024)S(1)} %broadcast_multiply_fusion.5) | copy-start | bytes 12292
  117.6 33.2 %copy-start.45 = (f32[1024]{0:T(1024)}, f32[1024]{0:T(1024)S(1)}, u32[]{:S(2)}) copy-start(f32[1024]{0:T(1024)S(1)} %add_rsqrt_fusion) | copy-start | bytes 12292
  142.6 93.0 %all-to-all-start = ((bf16[8,307,768]{2,1,0:T(8,128)(2,1)}), bf16[8,307,768]{2,1,0:T(8,128)(2,1)}, u32[]{:S(2)}, u32[]{:S(2)}) async-start(bf16[8,307,768]{2,1,0:T(8,128)(2,1)} %slice.59), calls=%async_computation | async-start | bytes 7667712 | tf_op jit(solution)/shard_map/all_to_all | solution.py:174
  150.0 180.0 %all-gather.3.cloned.1.call-start = ((), (), s32[]{:S(2)}) async-start(), calls=%async_computation.6 | async-start | bytes 5898240 | tf_op jit(solution)/shard_map/all_gather | solution.py:183
  235.6 89.4 %all-to-all-start.2 = ((bf16[8,307,768]{2,1,0:T(8,128)(2,1)}), bf16[8,307,768]{2,1,0:T(8,128)(2,1)}, u32[]{:S(2)}, u32[]{:S(2)}) async-start(bf16[8,307,768]{2,1,0:T(8,128)(2,1)} %slice.63), calls=%async_computation.2 | async-start | bytes 7667712 | tf_op jit(solution)/shard_map/all_to_all | solution.py:194
  240.1 110.3 %all-gather.5.cloned.1.call-start = ((), (), s32[]{:S(2)}) async-start(), calls=%async_computation.7 | async-start | bytes 5898240 | tf_op jit(solution)/shard_map/all_gather | solution.py:184
  379.4 89.8 %all-to-all-start.1 = ((bf16[8,307,768]{2,1,0:T(8,128)(2,1)}), bf16[8,307,768]{2,1,0:T(8,128)(2,1)}, u32[]{:S(2)}, u32[]{:S(2)}) async-start(bf16[8,307,768]{2,1,0:T(8,128)(2,1)} %reshape.360), calls=%async_computation.1 | async-start | bytes 7667712 | tf_op jit(solution)/shard_map/all_to_all | solution.py:193
  444.3 29.6 %copy-start.62 = (s32[2048,1]{0,1:T(1,128)S(1)}, s32[2048,1]{0,1:T(1,128)}, u32[]{:S(2)}) copy-start(s32[2048,1]{0,1:T(1,128)} %copy-done.61) | copy-start | bytes 24580
  444.3 29.7 %copy-start.13 = (bf16[1024,768]{1,0:T(8,128)(2,1)S(1)}, bf16[1024,768]{1,0:T(8,128)(2,1)}, u32[]{:S(2)}) copy-start(bf16[1024,768]{1,0:T(8,128)(2,1)} %param.33) | copy-start | bytes 4718596
  469.2 93.9 %all-to-all-start.3 = ((bf16[8,307,768]{2,1,0:T(8,128)(2,1)}), bf16[8,307,768]{2,1,0:T(8,128)(2,1)}, u32[]{:S(2)}, u32[]{:S(2)}) async-start(bf16[8,307,768]{2,1,0:T(8,128)(2,1)} %reshape.363), calls=%async_computation.3 | async-start | bytes 7667712 | tf_op jit(solution)/shard_map/all_to_all | solution.py:216
  473.8 531.6 %all-reduce.6.cloned.1.call-start = ((), (), s32[]{:S(2)}) async-start(), calls=%async_computation.10 | async-start | bytes 18874368 | tf_op jit(solution)/shard_map/psum | solution.py:304
  539.1 17.2 %copy-start.15 = (f32[1024,1,2]{2,1,0:T(1,128)S(1)}, f32[1024,1,2]{2,1,0:T(1,128)}, u32[]{:S(2)}) copy-start(f32[1024,1,2]{2,1,0:T(1,128)} %copy-done.14) | copy-start | bytes 24580
  539.1 17.2 %copy-start.49 = (f32[1024]{0:T(1024)S(1)}, f32[1024]{0:T(1024)}, u32[]{:S(2)}) copy-start(f32[1024]{0:T(1024)} %copy-done.48) | copy-start | bytes 12292
  539.1 18.2 %copy-start.23 = (s32[1024,2]{1,0:T(8,128)S(1)}, s32[1024,2]{1,0:T(8,128)}, u32[]{:S(2)}) copy-start(s32[1024,2]{1,0:T(8,128)} %copy-done.21) | copy-start | bytes 24580
  563.1 43.5 %copy-start.28 = (f32[1024,1,10]{2,1,0:T(1,128)}, f32[1024,1,10]{2,1,0:T(1,128)S(1)}, u32[]{:S(2)}) copy-start(f32[1024,1,10]{2,1,0:T(1,128)S(1)} %fusion.133) | copy-start | bytes 122884
  812.2 274.2 %reduce-scatter.3.cloned.1.call-start = ((), (), s32[]{:S(2)}) async-start(), calls=%async_computation.8 | async-start | bytes 11796480 | tf_op jit(solution)/shard_map/reduce_scatter | solution.py:301
  830.1 337.2 %reduce-scatter.5.cloned.1.call-start = ((), (), s32[]{:S(2)}) async-start(), calls=%async_computation.9 | async-start | bytes 11796480 | tf_op jit(solution)/shard_map/reduce_scatter | solution.py:302
  1005.4 165.2 %copy-start.27 = (f32[768,768]{1,0:T(8,128)S(1)}, f32[768,768]{1,0:T(8,128)}, u32[]{:S(2)}) copy-start(f32[768,768]{1,0:T(8,128)} %get-tuple-element.524) | copy-start | bytes 7077892
  (61 other events, 318.3 us)
Sparse Core Ops, SparseCore 0:
  152.4 38.8 all-gather.2
  242.5 38.7 all-gather.4
  812.3 192.9 all-reduce.5
  1008.4 77.9 reduce-scatter.2
  1089.4 77.8 reduce-scatter.4
where the time goes:
time: 1190 us; the launch traced here: 1180 us
  matrix products  407 us (34%)
  waiting for transfers between devices  374 us (31%)
  local copies, waits for them, and re-layouts  182 us (15%)
  other arithmetic  135 us (11%)
  blocking collectives  42 us (4%)
  starting transfers between devices  21.9 us (2%)
  between operations  15 us (1%)
    psum x1, waiting for transfers between devices, on_device(): lax.psum((gain_one_grad, w_query_grad, w_key_grad, w_value_grad, w_attn_o...  93.3 us
    reduce_scatter x1, waiting for transfers between devices, on_device(): lax.psum_scatter(w_in_grad[None], 'dp', scatter_dimension=1, tiled=True)  81 us
    reduce_scatter x1, waiting for transfers between devices, on_device(): lax.psum_scatter(w_out_grad[None], 'dp', scatter_dimension=1, tiled=True)  81 us
    all_to_all x1, waiting for transfers between devices, on_device(): lax.all_to_all(send_grads, 'expert', split_axis=0, concat_axis=0, tiled=T...  66.6 us
    dot_general x4, matrix products, block_scores(): jnp.einsum('qhd,khd->hqk', query_part, keys, preferred_element_type=jnp.f...  46.9 us
    convert_element_type x2, other arithmetic, attend_back(): score_grad = (probs * (prob_grad - delta)).astype(jnp.bfloat16)  42.4 us
    psum x1, blocking collectives, on_device(): lax.psum((gain_one_grad, w_query_grad, w_key_grad, w_value_grad, w_attn_o...  42 us
    dot_general x1, matrix products, on_device(): jnp.einsum('rd,fd->rf', flat_grads, pieces[1][0], preferred_element_type=...  37.1 us
  transfers between devices with their start and end apart: 9, of which 6 were waited for; matrix products, arithmetic and copies ran while one was open for 26% of the time, Pallas kernels for 0%

commit v1 on v0

v1 whole, which is shorter than its diff:
```python
import functools

import jax
import jax.numpy as jnp
from jax import lax
from jax.experimental import pallas as pl
from jax.experimental.pallas import tpu as pltpu
from jax.sharding import PartitionSpec as P

HEADS = 12
WINDOW = 512
F32 = jnp.float32
BF16 = jnp.bfloat16


highest = lax.Precision.HIGHEST
epsilon = 1e-05


def nt_dot(a, b):
    return lax.dot_general(a, b, (((1,), (1,)), ((), ())), preferred_element_type=F32)


def dot(a, b):
    return jnp.dot(a, b, preferred_element_type=F32)


def key_start(q_from, window):
    return max(0, q_from - window)


def fill_bias(first_ref, bias_ref, seq, block, window):
    for q_from in range(0, seq, block):
        low = key_start(q_from, window)
        size = q_from + block - low
        key = lax.broadcasted_iota(jnp.int32, (size, block), 0) + low
        place = lax.broadcasted_iota(jnp.int32, (size, block), 1) + q_from
        first = first_ref[0:1, q_from : q_from + block]
        keep = (key >= first) & (key <= place)
        bias_ref[0:size, q_from : q_from + block] = jnp.where(keep, 0.0, -1e9)


def attend_kernel(first_ref, q_ref, k_ref, v_ref, o_ref, lse_ref, bias_ref, vt_ref, ot_ref, *, block, window, scale):
    seq = q_ref.shape[0]
    half = q_ref.shape[1] // 2

    @pl.when(pl.program_id(0) == 0)
    def _():
        fill_bias(first_ref, bias_ref, seq, block, window)

    vt_ref[...] = v_ref[...].T
    lane = lax.broadcasted_iota(jnp.int32, (block, 2 * half), 1)
    for q_from in range(0, seq, block):
        low = key_start(q_from, window)
        high = q_from + block
        q_both = q_ref[q_from:high, :] * scale
        for head in range(2):
            q_one = jnp.where((lane < half) == (head == 0), q_both, jnp.zeros_like(q_both))
            scores = nt_dot(k_ref[low:high, :], q_one) + bias_ref[0 : high - low, q_from:high]
            top = jnp.max(scores, axis=0, keepdims=True)
            expd = jnp.exp(scores - top)
            total = jnp.sum(expd, axis=0, keepdims=True)
            mixed = dot(vt_ref[head * half : (head + 1) * half, low:high], expd.astype(BF16))
            ot_ref[head * half : (head + 1) * half, q_from:high] = mixed / total
            lse_ref[0, head : head + 1, q_from:high] = top + jnp.log(total)
    o_ref[...] = ot_ref[...].T.astype(BF16)


def attend(first, q, k, v, heads, window, block=256):
    seq, width = q.shape
    pair = 2 * width // heads
    col = pl.BlockSpec((seq, pair), lambda i: (0, i))
    return pl.pallas_call(
        functools.partial(attend_kernel, block=block, window=window, scale=(width // heads) ** -0.5),
        grid=(heads // 2,),
        in_specs=[pl.BlockSpec((1, seq), lambda i: (0, 0)), col, col, col],
        out_specs=[col, pl.BlockSpec((1, 8, seq), lambda i: (i, 0, 0))],
        out_shape=[
            jax.ShapeDtypeStruct((seq, width), BF16),
            jax.ShapeDtypeStruct((heads // 2, 8, seq), F32),
        ],
        scratch_shapes=[
            pltpu.VMEM((window + block, seq), F32),
            pltpu.VMEM((pair, seq), BF16),
            pltpu.VMEM((pair, seq), F32),
        ],
        compiler_params=pltpu.CompilerParams(vmem_limit_bytes=48 << 20),
        cost_estimate=pl.CostEstimate(flops=8 * seq * seq * width, bytes_accessed=8 * seq * width, transcendentals=seq * seq * heads),
        name="attend",
    )(first, q, k, v)


def attend_back_kernel(first_ref, lse_ref, q_ref, k_ref, v_ref, o_ref, do_ref, dq_ref, dk_ref, dv_ref, bias_ref, kt_ref, dqt_ref, delta_ref, dk_acc, dv_acc, *, block, window, scale):
    seq = q_ref.shape[0]
    half = q_ref.shape[1] // 2

    @pl.when(pl.program_id(0) == 0)
    def _():
        fill_bias(first_ref, bias_ref, seq, block, window)

    kt_ref[...] = k_ref[...].T
    both = (o_ref[...].astype(F32) * do_ref[...].astype(F32)).T
    delta_ref[0:1, :] = jnp.sum(both[0:half], axis=0, keepdims=True)
    delta_ref[1:2, :] = jnp.sum(both[half:], axis=0, keepdims=True)
    lane = lax.broadcasted_iota(jnp.int32, (block, 2 * half), 1)
    dk_acc[...] = jnp.zeros_like(dk_acc)
    dv_acc[...] = jnp.zeros_like(dv_acc)
    for q_from in range(0, seq, block):
        low = key_start(q_from, window)
        high = q_from + block
        q_both = q_ref[q_from:high, :] * scale
        do_both = do_ref[q_from:high, :]
        for head in range(2):
            mine = (lane < half) == (head == 0)
            q_one = jnp.where(mine, q_both, jnp.zeros_like(q_both))
            do_one = jnp.where(mine, do_both, jnp.zeros_like(do_both))
            scores = nt_dot(k_ref[low:high, :], q_one) + bias_ref[0 : high - low, q_from:high]
            probs = jnp.exp(scores - lse_ref[0, head : head + 1, q_from:high])
            prob_grad = nt_dot(v_ref[low:high, :], do_one)
            dv_acc[low:high, :] += dot(probs.astype(BF16), do_one)
            score_grad = (probs * (prob_grad - delta_ref[head : head + 1, q_from:high])).astype(BF16)
            dk_acc[low:high, :] += dot(score_grad, q_one)
            dqt_ref[head * half : (head + 1) * half, q_from:high] = dot(
                kt_ref[head * half : (head + 1) * half, low:high], score_grad
            )
    dq_ref[...] = (dqt_ref[...].T * scale).astype(BF16)
    dk_ref[...] = dk_acc[...].astype(BF16)
    dv_ref[...] = dv_acc[...].astype(BF16)


def attend_back(first, lse, q, k, v, o, do, heads, window, block=256):
    seq, width = q.shape
    pair = 2 * width // heads
    col = pl.BlockSpec((seq, pair), lambda i: (0, i))
    shape = jax.ShapeDtypeStruct((seq, width), BF16)
    return pl.pallas_call(
        functools.partial(attend_back_kernel, block=block, window=window, scale=(width // heads) ** -0.5),
        grid=(heads // 2,),
        in_specs=[
            pl.BlockSpec((1, seq), lambda i: (0, 0)),
            pl.BlockSpec((1, 8, seq), lambda i: (i, 0, 0)),
            col, col, col, col, col,
        ],
        out_specs=[col, col, col],
        out_shape=[shape, shape, shape],
        scratch_shapes=[
            pltpu.VMEM((window + block, seq), F32),
            pltpu.VMEM((pair, seq), BF16),
            pltpu.VMEM((pair, seq), F32),
            pltpu.VMEM((8, seq), F32),
            pltpu.VMEM((seq, pair), F32),
            pltpu.VMEM((seq, pair), F32),
        ],
        compiler_params=pltpu.CompilerParams(vmem_limit_bytes=48 << 20),
        cost_estimate=pl.CostEstimate(flops=20 * seq * seq * width, bytes_accessed=16 * seq * width, transcendentals=seq * seq * heads),
        name="attend_back",
    )(first, lse, q, k, v, o, do)


def gather_kernel(spots_ref, gates_ref, source_ref, rows_ref, *, first, capacity, gated):
    rows = rows_ref.shape[1]
    seq = source_ref.shape[0]
    slot = lax.broadcasted_iota(jnp.int32, (rows, seq), 0)
    slot = slot + (pl.program_id(0) + first) * capacity
    zero = slot == spots_ref[0:1, :]
    one = slot == spots_ref[1:2, :]
    taken = dot((zero | one).astype(BF16), source_ref[...])
    if gated:
        weight = jnp.where(zero, gates_ref[0:1, :], 0.0) + jnp.where(one, gates_ref[1:2, :], 0.0)
        taken = taken * jnp.sum(weight, axis=1, keepdims=True)
    rows_ref[0] = taken.astype(BF16)


def gather_rows(spots, gates, source, first, count, capacity, gated):
    seq, width = source.shape
    fixed = lambda i: (0, 0)
    return pl.pallas_call(
        functools.partial(gather_kernel, first=first, capacity=capacity, gated=gated),
        grid=(count,),
        in_specs=[
            pl.BlockSpec((2, seq), fixed),
            pl.BlockSpec((2, seq), fixed),
            pl.BlockSpec((seq, width), fixed),
        ],
        out_specs=pl.BlockSpec((1, capacity, width), lambda i: (i, 0, 0)),
        out_shape=jax.ShapeDtypeStruct((count, capacity, width), BF16),
        compiler_params=pltpu.CompilerParams(vmem_limit_bytes=40 << 20),
        cost_estimate=pl.CostEstimate(
            flops=2 * count * capacity * seq * width,
            bytes_accessed=2 * (count * capacity + seq) * width,
            transcendentals=0,
        ),
        name="gather_rows",
    )(spots, gates, source)


def normal_of(hidden):
    centre = hidden - jnp.mean(hidden, axis=-1, keepdims=True)
    inverse = lax.rsqrt(jnp.mean(centre * centre, axis=-1, keepdims=True) + epsilon)
    return centre * inverse, inverse


def pick_matrix(spot, first, rows):
    slot = lax.broadcasted_iota(jnp.int32, (spot.shape[0], rows), 1) + first
    return slot == spot


def combine_kernel(spots_ref, gates_ref, routes_ref, hidden_ref, dy_ref, gain_ref, frozen_ref, new_ref, out_ref, full_ref, gate_grad_ref, *, experts):
    frozen_rows, new_rows = frozen_ref.shape[0], new_ref.shape[0]
    hidden = hidden_ref[...]
    dy = dy_ref[...].astype(F32)
    picked = []
    terms = []
    for k in range(2):
        spot = spots_ref[:, k : k + 1]
        value = dot(pick_matrix(spot, 0, frozen_rows).astype(BF16), frozen_ref[...]) + dot(
            pick_matrix(spot, frozen_rows, new_rows).astype(BF16), new_ref[...]
        )
        picked.append(value)
        terms.append(jnp.sum(value * dy, axis=1, keepdims=True))
    gates = [gates_ref[:, k : k + 1] for k in range(2)]
    out_ref[...] = (hidden + (gates[0] * picked[0] + gates[1] * picked[1])).astype(BF16)
    inner = gates[0] * terms[0] + gates[1] * terms[1]
    expert = lax.broadcasted_iota(jnp.int32, (hidden.shape[0], experts), 1)
    full = jnp.zeros(expert.shape, F32)
    for k in range(2):
        full = full + jnp.where(expert == routes_ref[:, k : k + 1], gates[k] * (terms[k] - inner), 0.0)
    full_ref[...] = full
    norm_two = normal_of(hidden)[0] * gain_ref[...]

    @pl.when(pl.program_id(0) == 0)
    def _():
        gate_grad_ref[...] = jnp.zeros_like(gate_grad_ref)

    for e in range(experts):
        gate_grad_ref[e : e + 1, :] += jnp.sum(norm_two * full[:, e : e + 1], axis=0, keepdims=True)


def combine(spots, gates, routes, hidden, dy, gain, frozen_out, new_out, experts, block=256):
    seq, width = hidden.shape
    fixed = lambda i: (0, 0)
    moving = lambda i: (i, 0)
    return pl.pallas_call(
        functools.partial(combine_kernel, experts=experts),
        grid=(seq // block,),
        in_specs=[
            pl.BlockSpec((block, 2), moving),
            pl.BlockSpec((block, 2), moving),
            pl.BlockSpec((block, 2), moving),
            pl.BlockSpec((block, width), moving),
            pl.BlockSpec((block, width), moving),
            pl.BlockSpec((1, width), fixed),
            pl.BlockSpec(frozen_out.shape, fixed),
            pl.BlockSpec(new_out.shape, fixed),
        ],
        out_specs=[
            pl.BlockSpec((block, width), moving),
            pl.BlockSpec((block, experts), moving),
            pl.BlockSpec((experts, width), fixed),
        ],
        out_shape=[
            jax.ShapeDtypeStruct((seq, width), BF16),
            jax.ShapeDtypeStruct((seq, experts), F32),
            jax.ShapeDtypeStruct((experts, width), F32),
        ],
        compiler_params=pltpu.CompilerParams(vmem_limit_bytes=48 << 20),
        cost_estimate=pl.CostEstimate(
            flops=4 * seq * (frozen_out.shape[0] + new_out.shape[0]) * width,
            bytes_accessed=16 * seq * width,
            transcendentals=0,
        ),
        name="combine",
    )(spots, gates, routes, hidden, dy, gain, frozen_out, new_out)


def combine_back_kernel(spots_ref, full_ref, hidden_ref, dy_ref, gain_ref, w_gate_ref, frozen_ref, new_ref, grad_ref, branch_ref, gain_grad_ref):
    frozen_rows, new_rows = frozen_ref.shape[0], new_ref.shape[0]
    spot_zero, spot_one = spots_ref[:, 0:1], spots_ref[:, 1:2]

    def both(first, rows):
        return (pick_matrix(spot_zero, first, rows) | pick_matrix(spot_one, first, rows)).astype(BF16)

    upstream = dot(both(0, frozen_rows), frozen_ref[...]) + dot(both(frozen_rows, new_rows), new_ref[...])
    full = full_ref[...]
    for e in range(w_gate_ref.shape[0]):
        upstream = upstream + full[:, e : e + 1] * w_gate_ref[e : e + 1, :]
    normal, inverse = normal_of(hidden_ref[...])

    @pl.when(pl.program_id(0) == 0)
    def _():
        gain_grad_ref[...] = jnp.zeros_like(gain_grad_ref)

    gain_grad_ref[...] += jnp.sum(upstream * normal, axis=0, keepdims=True)
    scaled = upstream * gain_ref[...]
    inner = (
        scaled
        - jnp.mean(scaled, axis=-1, keepdims=True)
        - normal * jnp.mean(scaled * normal, axis=-1, keepdims=True)
    )
    grad = dy_ref[...].astype(F32) + inner * inverse
    grad_ref[...] = grad
    branch_ref[...] = grad.astype(BF16)


def combine_back(spots, full, hidden, dy, gain, w_gate_t, frozen_back, new_back, block=256):
    seq, width = hidden.shape
    experts = w_gate_t.shape[0]
    fixed = lambda i: (0, 0)
    moving = lambda i: (i, 0)
    return pl.pallas_call(
        combine_back_kernel,
        grid=(seq // block,),
        in_specs=[
            pl.BlockSpec((block, 2), moving),
            pl.BlockSpec((block, experts), moving),
            pl.BlockSpec((block, width), moving),
            pl.BlockSpec((block, width), moving),
            pl.BlockSpec((1, width), fixed),
            pl.BlockSpec((experts, width), fixed),
            pl.BlockSpec(frozen_back.shape, fixed),
            pl.BlockSpec(new_back.shape, fixed),
        ],
        out_specs=[
            pl.BlockSpec((block, width), moving),
            pl.BlockSpec((block, width), moving),
            pl.BlockSpec((1, width), fixed),
        ],
        out_shape=[
            jax.ShapeDtypeStruct((seq, width), F32),
            jax.ShapeDtypeStruct((seq, width), BF16),
            jax.ShapeDtypeStruct((1, width), F32),
        ],
        compiler_params=pltpu.CompilerParams(vmem_limit_bytes=48 << 20),
        cost_estimate=pl.CostEstimate(
            flops=2 * seq * (frozen_back.shape[0] + new_back.shape[0]) * width,
            bytes_accessed=16 * seq * width,
            transcendentals=0,
        ),
        name="combine_back",
    )(spots, full, hidden, dy, gain, w_gate_t, frozen_back, new_back)


def norm_backward(upstream, gain, normal_part, scale_inv):
    scaled = upstream * gain
    inner = (
        scaled
        - jnp.mean(scaled, axis=-1, keepdims=True)
        - normal_part * jnp.mean(scaled * normal_part, axis=-1, keepdims=True)
    )
    return inner * scale_inv


def first_keys(length_row, seq_len):
    ends = jnp.cumsum(length_row)
    places = jnp.arange(seq_len, dtype=jnp.int32)
    passed = places[None, :] >= ends[:, None]
    return jnp.max(jnp.where(passed, ends[:, None], 0), axis=0, keepdims=True)


def slot_spots(routes, experts, capacity):
    names = jnp.arange(experts, dtype=jnp.int32)[None, :]
    zero, one = routes[:, 0:1] == names, routes[:, 1:2] == names
    picks = (zero | one).astype(jnp.int32)
    earlier = jnp.cumsum(picks, axis=0) - picks
    ranks = [jnp.sum(jnp.where(mine, earlier, 0), axis=1, keepdims=True) for mine in (zero, one)]
    return routes * capacity + jnp.concatenate(ranks, axis=1), zero, one


def gelu_grad(pre, upstream):
    return jax.vjp(jax.nn.gelu, pre)[1](upstream)[0]


def expert_forward(rows, w_in_full, w_out_full):
    pre = jnp.einsum("rd,fd->rf", rows, w_in_full, preferred_element_type=F32)
    act = jax.nn.gelu(pre).astype(BF16)
    return dot(act, w_out_full).astype(BF16), pre, act


def expert_backward(grads, pre, w_in_full, w_out_full):
    act_grad = jnp.einsum("rd,fd->rf", grads, w_out_full, preferred_element_type=F32)
    pre_grad = gelu_grad(pre, act_grad).astype(BF16)
    return dot(pre_grad, w_in_full).astype(BF16), pre_grad


def transposed_dot(a, b):
    return jnp.einsum("td,te->de", a, b, preferred_element_type=F32)


def on_device(
    tokens,
    lengths,
    routes,
    gain_one,
    w_query,
    w_key,
    w_value,
    w_attn_out,
    gain_two,
    w_gate,
    frozen_in,
    frozen_out,
    new_in,
    new_out,
    out_grad,
):
    seq_len, width = tokens.shape
    experts = w_gate.shape[1]
    frozen = frozen_in.shape[0]
    new = experts - frozen
    capacity = -(-max(2, 3 * seq_len // experts) // 8) * 8
    exchange = functools.partial(
        lax.all_to_all, axis_name="expert", split_axis=0, concat_axis=0, tiled=True
    )
    w_in = lax.all_gather(new_in, "dp", axis=1, tiled=True)[0]
    w_out = lax.all_gather(new_out, "dp", axis=1, tiled=True)[0]

    x_in = tokens.astype(F32)
    normal_one, inv_one = normal_of(x_in)
    normed = (normal_one * gain_one).astype(BF16)
    query, keys, values = [dot(normed, w).astype(BF16) for w in (w_query, w_key, w_value)]
    first = first_keys(lengths[0], seq_len)
    mixed, log_totals = attend(first, query, keys, values, HEADS, WINDOW)
    hidden = x_in + dot(mixed, w_attn_out)
    norm_two = normal_of(hidden)[0] * gain_two
    norm_low = norm_two.astype(BF16)
    spots, zero, one = slot_spots(routes, experts, capacity)
    spots_row = spots.T
    rows_new = gather_rows(
        spots_row, jnp.zeros((2, seq_len), F32), norm_low, frozen, new, capacity, False
    )
    arrived = exchange(rows_new).reshape(-1, width)

    logits = jnp.dot(norm_two, w_gate, precision=highest)
    chosen = jnp.concatenate(
        [jnp.sum(jnp.where(mine, logits, 0.0), axis=1, keepdims=True) for mine in (zero, one)],
        axis=1,
    )
    weights = jnp.exp(chosen - jnp.max(chosen, axis=1, keepdims=True))
    gates = weights / jnp.sum(weights, axis=1, keepdims=True)
    gates_row = gates.T
    grads_new = gather_rows(spots_row, gates_row, out_grad, frozen, new, capacity, True)
    arrived_grads = exchange(grads_new).reshape(-1, width)
    rows_frozen = gather_rows(spots_row, gates_row, norm_low, 0, frozen, capacity, False)
    grads_frozen = gather_rows(spots_row, gates_row, out_grad, 0, frozen, capacity, True)
    frozen_outputs, frozen_back = [], []
    for e in range(frozen):
        produced, pre, _ = expert_forward(rows_frozen[e], frozen_in[e], frozen_out[e])
        back, _ = expert_backward(grads_frozen[e], pre, frozen_in[e], frozen_out[e])
        frozen_outputs.append(produced)
        frozen_back.append(back)
    frozen_outputs = jnp.concatenate(frozen_outputs, axis=0)
    frozen_back = jnp.concatenate(frozen_back, axis=0)

    produced, pre, act = expert_forward(arrived, w_in, w_out)
    returned = exchange(produced.reshape(new, capacity, width)).reshape(-1, width)
    rows_back, pre_grad = expert_backward(arrived_grads, pre, w_in, w_out)
    returned_back = exchange(rows_back.reshape(new, capacity, width)).reshape(-1, width)
    w_in_grad = jnp.einsum("rf,rd->fd", pre_grad, arrived, preferred_element_type=F32)
    w_out_grad = jnp.einsum("rf,rd->fd", act, arrived_grads, preferred_element_type=F32)
    new_in_grad = lax.psum_scatter(
        w_in_grad.astype(BF16)[None], "dp", scatter_dimension=1, tiled=True
    )
    new_out_grad = lax.psum_scatter(
        w_out_grad.astype(BF16)[None], "dp", scatter_dimension=1, tiled=True
    )

    output, full_logit_grad, w_gate_grad = combine(
        spots, gates, routes, hidden, out_grad, gain_two[None], frozen_outputs, returned, experts
    )
    hidden_grad, branch_grad, gain_two_grad = combine_back(
        spots, full_logit_grad, hidden, out_grad, gain_two[None], w_gate.T, frozen_back, returned_back
    )
    mixed_grad = jnp.einsum("te,de->td", branch_grad, w_attn_out, preferred_element_type=F32)
    w_attn_out_grad = transposed_dot(mixed, branch_grad)
    small = -(-(experts + 1) // 16) * 16
    early = jnp.concatenate(
        [
            w_attn_out_grad,
            w_gate_grad,
            gain_two_grad,
            jnp.zeros((small - experts - 1, width), F32),
        ],
        axis=0,
    ).astype(BF16)
    early = lax.psum(early, ("dp", "expert"))
    query_grad, key_grad, value_grad = attend_back(
        first, log_totals, query, keys, values, mixed, mixed_grad.astype(BF16), HEADS, WINDOW
    )
    late = jnp.concatenate(
        [transposed_dot(normed, g) for g in (query_grad, key_grad, value_grad)], axis=0
    ).astype(BF16)
    late, early = lax.optimization_barrier((late, early))
    late = lax.psum(late, ("dp", "expert")).astype(F32).reshape(3, width, width)
    early = early.astype(F32)
    normed_grad = sum(
        jnp.einsum("te,de->td", g, w, preferred_element_type=F32)
        for g, w in ((query_grad, w_query), (key_grad, w_key), (value_grad, w_value))
    )
    x_grad = hidden_grad + norm_backward(normed_grad, gain_one, normal_one, inv_one)
    gain_one_grad = (
        sum(
            jnp.sum(late[i] * w.astype(F32), axis=1)
            for i, w in enumerate((w_query, w_key, w_value))
        )
        / gain_one
    )
    return (
        output,
        x_grad,
        gain_one_grad,
        late[0],
        late[1],
        late[2],
        early[:width],
        early[width + experts],
        early[width : width + experts].T,
        new_in_grad.astype(F32),
        new_out_grad.astype(F32),
    )


def solution(mesh):
    return jax.shard_map(
        on_device,
        mesh=mesh,
        in_specs=(
            P(("dp", "expert"), None),
            P(("dp", "expert"), None),
            P(("dp", "expert"), None),
            P(),
            P(),
            P(),
            P(),
            P(),
            P(),
            P(),
            P(),
            P(),
            P("expert", "dp", None),
            P("expert", "dp", None),
            P(("dp", "expert"), None),
        ),
        out_specs=(
            P(("dp", "expert"), None),
            P(("dp", "expert"), None),
            P(),
            P(),
            P(),
            P(),
            P(),
            P(),
            P(),
            P("expert", "dp", None),
            P("expert", "dp", None),
        ),
        check_vma=False,
    )
```

time: 1190 us -> 841 us (0.71)
  matrix products: 407 us -> 206 us
  local copies, waits for them, and re-layouts: 182 us -> 22.3 us
  other arithmetic: 135 us -> 28.8 us
  Pallas kernels: 0 us -> 96.6 us
  waiting for transfers between devices: 374 us -> 442 us
  blocking collectives: 42 us -> 0 us
    dot_general x42 -> x24, matrix products: 403 us -> 200 us  [the longest x10 71.4 us: dot(): return jnp.dot(a, b, preferred_element_type=F32)]
    psum x1 -> x2, waiting for transfers between devices: 93.3 us -> 195 us  [the longest x1 99.8 us: on_device(): early = lax.psum(early, ('dp', 'expert'))]
    pallas_call x0 -> x8, Pallas kernels: none -> 96.6 us  [the longest x1 24.8 us: attend(): pl.pallas_call(functools.partial(attend_kernel, block=block, window=windo...]
    reduce_scatter x2, waiting for transfers between devices: 162 us -> 91 us  [the longest x1 47.5 us: on_device(): lax.psum_scatter(w_out_grad.astype(BF16)[None], 'dp', scatter_dimension=1...]
    gather x4 -> x0, local copies, waits for them, and re-layouts: 57 us -> none  [the longest x1 16.8 us: on_device(): jnp.concatenate([choice_grads, zero_row], axis=0)[owners]]
    reduce_sum x10 -> x5, other arithmetic: 57.2 us -> 8.72 us  [the longest x1 5.9 us: on_device(): jnp.sum(late[i] * w.astype(F32), axis=1)]
    convert_element_type x8 -> x5, other arithmetic: 51.3 us -> 6.31 us  [the longest x1 2.85 us: on_device(): new_in_grad.astype(F32)]
    psum x1 -> x0, blocking collectives: 42 us -> none  [on_device(): lax.psum((gain_one_grad, w_query_grad, w_key_grad, w_value_grad, w_attn_o...]
  transfers between devices with their start and end apart: 9 -> 10, of which waited for: 6 -> 8; matrix products, arithmetic and copies ran while one was open for 26% -> 28% of each run, Pallas kernels for 0% -> 10%
where the time goes in v1:
time: 841 us; the launch traced here: 832 us
  waiting for transfers between devices  442 us (53%)
  matrix products  206 us (24%)
  Pallas kernels  96.6 us (11%)
  other arithmetic  28.8 us (3%)
  local copies, waits for them, and re-layouts  22.3 us (3%)
  starting transfers between devices  21.8 us (3%)
  between operations  15.3 us (2%)
    psum x1, waiting for transfers between devices, on_device(): early = lax.psum(early, ('dp', 'expert'))  99.8 us
    psum x1, waiting for transfers between devices, on_device(): late = lax.psum(late, ('dp', 'expert')).astype(F32).reshape(3, width, width)  95.4 us
    dot_general x10, matrix products, dot(): return jnp.dot(a, b, preferred_element_type=F32)  71.4 us
    all_to_all x1, waiting for transfers between devices, on_device(): arrived = exchange(rows_new).reshape(-1, width)  70.6 us
    reduce_scatter x1, waiting for transfers between devices, on_device(): lax.psum_scatter(w_out_grad.astype(BF16)[None], 'dp', scatter_dimension=1...  47.5 us
    reduce_scatter x1, waiting for transfers between devices, on_device(): lax.psum_scatter(w_in_grad.astype(BF16)[None], 'dp', scatter_dimension=1,...  43.4 us
    dot_general x3, matrix products, expert_forward(): pre = jnp.einsum('rd,fd->rf', rows, w_in_full, preferred_element_type=F32)  38.7 us
    dot_general x1, matrix products, expert_backward(): jnp.einsum('rd,fd->rf', grads, w_out_full, preferred_element_type=F32)  37.4 us
  transfers between devices with their start and end apart: 10, of which 8 were waited for; matrix products, arithmetic and copies ran while one was open for 28% of the time, Pallas kernels for 10%

profile of v1, /device:TPU:0, one launch (start us, length us, event | category | flops | bytes accessed | tf_op | source)
XLA Modules:
  0.0 832.0 jit_solution(11316085163669054850)
XLA Ops:
  26.3 24.8 %attend.1 = (bf16[1024,768]{1,0:T(8,128)(2,1)S(1)}, f32[6,8,1024]{2,1,0:T(8,128)S(1)}) custom-call(s32[1,1024]{1,0:T(1,128)S(1)} %bitcast.128, bf16[1024,768]{1,0:T(8,128)(2,1)S(1)} %convolution_convert_fusion.7.q_ref, bf16[1024,768]{1,0:T(8,128)(2,1)S(1)} %convolution_convert_fusion.6.k_ref, bf16[1024,768]{1,0:T(8,128)(2,1)} %convolution_convert_fusion.5.v_ref), custom_call_target="tpu_custom_call" | custom-call | flops 6442450944 | bytes 6291456 | tf_op jit(solution)/shard_map/attend/pallas_call | solution.py:73
  54.4 6.0 gather_rows.5
  63.4 7.3 all-to-all-start
  76.7 7.2 gather_rows.7
  85.9 70.6 %all-to-all-done = bf16[8,312,768]{2,1,0:T(8,128)(2,1)} async-done(((bf16[8,312,768]{2,1,0:T(8,128)(2,1)}), bf16[8,312,768]{2,1,0:T(8,128)(2,1)}, u32[]{:S(2)}, u32[]{:S(2)}) %all-to-all-start) | async-done | bytes 3833888 | tf_op jit(solution)/shard_map/all_to_all | solution.py:431
  161.7 28.8 %multiply_convert_fusion = (bf16[2496,3072]{1,0:T(8,128)(2,1)}, f32[2496,3072]{1,0:T(8,128)}) fusion(bf16[2496,768]{1,0:T(8,128)(2,1)} %bitcast.21, bf16[1,3072,768]{2,1,0:T(8,128)(2,1)} %all-gather.3.cloned.1.call-done), kind=kOutput, calls=%fused_computation.9 | convolution fusion | flops 11846615040 | bytes 54558720 | tf_op jit(solution)/shard_map/rd,fd->rf/dot_general | solution.py:374
  190.5 18.1 %convolution_convert_fusion.3 = bf16[2496,768]{1,0:T(8,128)(2,1)} fusion(bf16[2496,3072]{1,0:T(8,128)(2,1)} %get-tuple-element.57, bf16[1,3072,768]{2,1,0:T(8,128)(2,1)} %all-gather.5.cloned.1.call-done), kind=kOutput, calls=%fused_computation.17 | convolution fusion | flops 11779522560 | bytes 23887872 | tf_op jit(solution)/shard_map/dot_general | solution.py:25
  208.6 37.2 %all-to-all-done.2 = bf16[8,312,768]{2,1,0:T(8,128)(2,1)} async-done(((bf16[8,312,768]{2,1,0:T(8,128)(2,1)}), bf16[8,312,768]{2,1,0:T(8,128)(2,1)}, u32[]{:S(2)}, u32[]{:S(2)}) %all-to-all-start.2) | async-done | bytes 3833888 | tf_op jit(solution)/shard_map/all_to_all | solution.py:442
  250.6 37.4 %fusion.6 = bf16[2496,3072]{1,0:T(8,128)(2,1)} fusion(f32[2496,3072]{1,0:T(8,128)} %get-tuple-element.58, bf16[2496,768]{1,0:T(8,128)(2,1)} %bitcast.29, bf16[1,3072,768]{2,1,0:T(8,128)(2,1)} %all-gather.5.cloned.1.call-done), kind=kOutput, calls=%fused_computation.8 | convolution fusion | flops 11930959872 | bytes 54558720 | tf_op jit(solution)/shard_map/rd,fd->rf/dot_general | solution.py:380
  287.9 18.3 %convolution_convert_fusion.2 = bf16[2496,768]{1,0:T(8,128)(2,1)} fusion(bf16[2496,3072]{1,0:T(8,128)(2,1)} %fusion.6, bf16[1,3072,768]{2,1,0:T(8,128)(2,1)} %all-gather.3.cloned.1.call-done), kind=kOutput, calls=%fused_computation.16 | convolution fusion | flops 11779522560 | bytes 23887872 | tf_op jit(solution)/shard_map/dot_general | solution.py:25
  306.3 29.1 %all-to-all-done.1 = bf16[8,312,768]{2,1,0:T(8,128)(2,1)} async-done(((bf16[8,312,768]{2,1,0:T(8,128)(2,1)}), bf16[8,312,768]{2,1,0:T(8,128)(2,1)}, u32[]{:S(2)}, u32[]{:S(2)}) %all-to-all-start.1) | async-done | bytes 3833888 | tf_op jit(solution)/shard_map/all_to_all | solution.py:455
  363.4 10.0 %fusion.86 = bf16[312,768]{1,0:T(8,128)(2,1)} fusion(bf16[2,3072,768]{2,1,0:T(8,128)(2,1)} %param.25, f32[312,3072]{1,0:T(8,128)} %copy-done.57, bf16[2,3072,768]{2,1,0:T(8,128)(2,1)} %param.26, bf16[2,312,768]{2,1,0:T(8,128)(2,1)S(1)} %copy-done.22), kind=kOutput, calls=%fused_computation.109 | convolution fusion | flops 2963810304 | bytes 14229504 | tf_op jit(solution)/shard_map/dot_general | solution.py:25
  373.4 10.1 %fusion.89 = bf16[312,768]{1,0:T(8,128)(2,1)} fusion(bf16[2,3072,768]{2,1,0:T(8,128)(2,1)} %param.25, f32[312,3072]{1,0:T(8,128)} %copy-done.56, bf16[2,3072,768]{2,1,0:T(8,128)(2,1)} %param.26, bf16[2,312,768]{2,1,0:T(8,128)(2,1)S(1)} %copy-done.22), kind=kOutput, calls=%fused_computation.110 | convolution fusion | flops 2963810304 | bytes 14229504 | tf_op jit(solution)/shard_map/dot_general | solution.py:25
  388.4 18.3 %combine.1 = (bf16[1024,768]{1,0:T(8,128)(2,1)}, f32[1024,10]{1,0:T(8,128)S(1)}, f32[10,768]{1,0:T(8,128)S(1)}) custom-call(s32[1024,2]{1,0:T(8,128)S(1)} %add.72.spots_ref, f32[1024,2]{1,0:T(8,128)S(1)} %copy-done.6, s32[1024,2]{1,0:T(8,128)S(1)} %copy.94.routes_ref, f32[1024,768]{1,0:T(8,128)} %copy-done.32, bf16[1024,768]{1,0:T(8,128)(2,1)S(1)} %copy-done.17, ...), custom_call_target="tpu_custom_call" | custom-call | flops 9814671360 | bytes 12582912 | tf_op jit(solution)/shard_map/combine/pallas_call | solution.py:243
  407.5 17.5 %all-to-all-done.3 = bf16[8,312,768]{2,1,0:T(8,128)(2,1)} async-done(((bf16[8,312,768]{2,1,0:T(8,128)(2,1)}), bf16[8,312,768]{2,1,0:T(8,128)(2,1)}, u32[]{:S(2)}, u32[]{:S(2)}) %all-to-all-start.3) | async-done | bytes 3833888 | tf_op jit(solution)/shard_map/all_to_all | solution.py:457
  427.4 13.8 %combine_back.1 = (f32[1024,768]{1,0:T(8,128)}, bf16[1024,768]{1,0:T(8,128)(2,1)S(1)}, f32[1,768]{1,0:T(1,128)S(1)}) custom-call(s32[1024,2]{1,0:T(8,128)S(1)} %add.72.spots_ref, f32[1024,10]{1,0:T(8,128)S(1)} %copy-done.31, f32[1024,768]{1,0:T(8,128)} %copy-done.32, bf16[1024,768]{1,0:T(8,128)(2,1)S(1)} %copy-done.18, ...), custom_call_target="tpu_custom_call" | custom-call | flops 4907335680 | bytes 12582912 | tf_op jit(solution)/shard_map/combine_back/pallas_call | solution.py:310
  446.7 22.8 %attend_back.1 = (bf16[1024,768]{1,0:T(8,128)(2,1)S(1)}, bf16[1024,768]{1,0:T(8,128)(2,1)S(1)}, bf16[1024,768]{1,0:T(8,128)(2,1)S(1)}) custom-call(s32[1,1024]{1,0:T(1,128)S(1)} %bitcast.129, f32[6,8,1024]{2,1,0:T(8,128)S(1)} %get-tuple-element.28.lse_ref, bf16[1024,768]{1,0:T(8,128)(2,1)} %copy-done.29, bf16[1024,768]{1,0:T(8,128)(2,1)} %copy-done.28, ...), custom_call_target="tpu_custom_call" | custom-call | flops 16106127360 | bytes 12582912 | tf_op jit(solution)/shard_map/attend_back/pallas_call | solution.py:136
  476.7 99.8 %all-reduce.3.cloned.1.call-done = bf16[784,768]{1,0:T(8,128)(2,1)} async-done(((bf16[784,768]{1,0:T(8,128)(2,1)}), bf16[784,768]{1,0:T(8,128)(2,1)}) %all-reduce.3.cloned.1.call-update) | async-done | bytes 1204240 | tf_op jit(solution)/shard_map/psum | solution.py:485
  576.5 18.5 %fusion.28 = bf16[1,3072,768]{2,1,0:T(8,128)(2,1)} fusion(bf16[2496,3072]{1,0:T(8,128)(2,1)} %fusion.6, bf16[2496,768]{1,0:T(8,128)(2,1)} %bitcast.21), kind=kOutput, calls=%fused_computation.42 | convolution fusion | flops 11779964928 | bytes 23887872 | tf_op jit(solution)/shard_map/rf,rd->fd/dot_general | solution.py:458
  595.1 18.8 %fusion.29 = bf16[1,3072,768]{2,1,0:T(8,128)(2,1)} fusion(bf16[2496,3072]{1,0:T(8,128)(2,1)} %get-tuple-element.57, bf16[2496,768]{1,0:T(8,128)(2,1)} %bitcast.29), kind=kOutput, calls=%fused_computation.43 | convolution fusion | flops 11779964928 | bytes 23887872 | tf_op jit(solution)/shard_map/rf,rd->fd/dot_general | solution.py:459
  626.4 95.4 %all-reduce.5.cloned.1.call-done = bf16[2304,768]{1,0:T(8,128)(2,1)} async-done(((bf16[2304,768]{1,0:T(8,128)(2,1)}), bf16[2304,768]{1,0:T(8,128)(2,1)}) %all-reduce.5.cloned.1.call-update) | async-done | bytes 3538960 | tf_op jit(solution)/shard_map/psum | solution.py:493
  721.8 5.9 multiply_reduce_fusion.2
  728.3 43.4 %reduce-scatter.3.cloned.1.call-done = bf16[1,768,768]{2,1,0:T(8,128)(2,1)} async-done(((bf16[1,3072,768]{2,1,0:T(8,128)(2,1)}), bf16[1,768,768]{2,1,0:T(8,128)(2,1)}) %reduce-scatter.3.cloned.1.call-update) | async-done | bytes 1179664 | tf_op jit(solution)/shard_map/reduce_scatter | solution.py:460
  774.6 47.5 %reduce-scatter.5.cloned.1.call-done = bf16[1,768,768]{2,1,0:T(8,128)(2,1)} async-done(((bf16[1,3072,768]{2,1,0:T(8,128)(2,1)}), bf16[1,768,768]{2,1,0:T(8,128)(2,1)}) %reduce-scatter.5.cloned.1.call-update) | async-done | bytes 1179664 | tf_op jit(solution)/shard_map/reduce_scatter | solution.py:463
  (212 shorter events, 110.0 us)
Async XLA Ops:
  7.2 44.0 %copy-start = (bf16[768,768]{1,0:T(8,128)(2,1)S(1)}, bf16[768,768]{1,0:T(8,128)(2,1)}, u32[]{:S(2)}) copy-start(bf16[768,768]{1,0:T(8,128)(2,1)} %param.22) | copy-start | bytes 3538948
  7.2 154.4 %all-gather.3.cloned.1.call-start = ((), (), s32[]{:S(2)}) async-start(), calls=%async_computation.6 | async-start | bytes 5898240 | tf_op jit(solution)/shard_map/all_gather | solution.py:414
  9.7 15.0 %copy-start.45 = (f32[1024]{0:T(1024)}, f32[1024]{0:T(1024)S(1)}, u32[]{:S(2)}) copy-start(f32[1024]{0:T(1024)S(1)} %broadcast_multiply_fusion.4) | copy-start | bytes 12292
  10.3 14.3 %copy-start.47 = (f32[1024]{0:T(1024)}, f32[1024]{0:T(1024)S(1)}, u32[]{:S(2)}) copy-start(f32[1024]{0:T(1024)S(1)} %add_rsqrt_fusion.1) | copy-start | bytes 12292
  21.5 55.2 %copy-start.9 = (s32[2,1024]{1,0:T(2,128)}, s32[2,1024]{1,0:T(2,128)S(1)}, u32[]{:S(2)}) copy-start(s32[2,1024]{1,0:T(2,128)S(1)} %copy.91.spots_ref) | copy-start | bytes 24580
  26.3 24.9 %copy-start.29 = (bf16[1024,768]{1,0:T(8,128)(2,1)}, bf16[1024,768]{1,0:T(8,128)(2,1)S(1)}, u32[]{:S(2)}) copy-start(bf16[1024,768]{1,0:T(8,128)(2,1)S(1)} %convolution_convert_fusion.7.q_ref) | copy-start | bytes 4718596
  63.4 93.0 %all-to-all-start = ((bf16[8,312,768]{2,1,0:T(8,128)(2,1)}), bf16[8,312,768]{2,1,0:T(8,128)(2,1)}, u32[]{:S(2)}, u32[]{:S(2)}) async-start(bf16[8,312,768]{2,1,0:T(8,128)(2,1)} %copy-done.1), calls=%async_computation | async-start | bytes 7667712 | tf_op jit(solution)/shard_map/all_to_all | solution.py:431
  70.7 119.8 %all-gather.5.cloned.1.call-start = ((), (), s32[]{:S(2)}) async-start(), calls=%async_computation.7 | async-start | bytes 5898240 | tf_op jit(solution)/shard_map/all_gather | solution.py:415
  156.5 89.4 %all-to-all-start.2 = ((bf16[8,312,768]{2,1,0:T(8,128)(2,1)}), bf16[8,312,768]{2,1,0:T(8,128)(2,1)}, u32[]{:S(2)}, u32[]{:S(2)}) async-start(bf16[8,312,768]{2,1,0:T(8,128)(2,1)} %copy-done.2), calls=%async_computation.2 | async-start | bytes 7667712 | tf_op jit(solution)/shard_map/all_to_all | solution.py:442
  245.9 89.5 %all-to-all-start.1 = ((bf16[8,312,768]{2,1,0:T(8,128)(2,1)}), bf16[8,312,768]{2,1,0:T(8,128)(2,1)}, u32[]{:S(2)}, u32[]{:S(2)}) async-start(bf16[8,312,768]{2,1,0:T(8,128)(2,1)} %bitcast.131), calls=%async_computation.1 | async-start | bytes 7667712 | tf_op jit(solution)/shard_map/all_to_all | solution.py:455
  335.4 89.5 %all-to-all-start.3 = ((bf16[8,312,768]{2,1,0:T(8,128)(2,1)}), bf16[8,312,768]{2,1,0:T(8,128)(2,1)}, u32[]{:S(2)}, u32[]{:S(2)}) async-start(bf16[8,312,768]{2,1,0:T(8,128)(2,1)} %bitcast.130), calls=%async_computation.3 | async-start | bytes 7667712 | tf_op jit(solution)/shard_map/all_to_all | solution.py:457
  340.1 236.3 %all-reduce.3.cloned.1.call-start = ((), (), s32[]{:S(2)}) async-start(), calls=%async_computation.8 | async-start | bytes 2408448 | tf_op jit(solution)/shard_map/psum | solution.py:485
  347.6 9.9 %slice-start = ((s8[9437184]{0:T(1024)(128)(4,1)}), s8[4194304]{0:T(1024)(128)(4,1)S(1)}, s32[]{:S(2)}) async-start(s8[9437184]{0:T(1024)(128)(4,1)} %bitcast.150), calls=%async_computation.12 | async-start | bytes 8388608
  388.4 36.5 %copy-start.8 = (f32[768,10]{0,1:T(8,128)S(1)}, f32[768,10]{0,1:T(8,128)}, u32[]{:S(2)}) copy-start(f32[768,10]{0,1:T(8,128)} %param.24) | copy-start | bytes 92164
  427.4 13.8 %copy-start.24 = (bf16[1024,768]{1,0:T(8,128)(2,1)S(1)}, bf16[1024,768]{1,0:T(8,128)(2,1)}, u32[]{:S(2)}) copy-start(bf16[1024,768]{1,0:T(8,128)(2,1)} %copy-done.23) | copy-start | bytes 4718596
  446.6 275.3 %all-reduce.5.cloned.1.call-start = ((), (), s32[]{:S(2)}) async-start(), calls=%async_computation.9 | async-start | bytes 7077888 | tf_op jit(solution)/shard_map/psum | solution.py:493
  446.6 22.9 %copy-start.34 = (bf16[1024,768]{1,0:T(8,128)(2,1)S(1)}, bf16[1024,768]{1,0:T(8,128)(2,1)}, u32[]{:S(2)}) copy-start(bf16[1024,768]{1,0:T(8,128)(2,1)} %param.15) | copy-start | bytes 4718596
  446.6 22.9 %copy-start.46 = (f32[1024]{0:T(1024)S(1)}, f32[1024]{0:T(1024)}, u32[]{:S(2)}) copy-start(f32[1024]{0:T(1024)} %copy-done.45) | copy-start | bytes 12292
  446.6 22.9 %copy-start.48 = (f32[1024]{0:T(1024)S(1)}, f32[1024]{0:T(1024)}, u32[]{:S(2)}) copy-start(f32[1024]{0:T(1024)} %copy-done.47) | copy-start | bytes 12292
  446.6 22.9 %copy-start.54 = (f32[768]{0:T(1024)S(1)}, f32[768]{0:T(1024)}, u32[]{:S(2)}) copy-start(f32[768]{0:T(1024)} %param.18) | copy-start | bytes 9220
  576.5 195.3 %reduce-scatter.3.cloned.1.call-start = ((), (), s32[]{:S(2)}) async-start(), calls=%async_computation.10 | async-start | bytes 5898240 | tf_op jit(solution)/shard_map/reduce_scatter | solution.py:460
  595.0 227.1 %reduce-scatter.5.cloned.1.call-start = ((), (), s32[]{:S(2)}) async-start(), calls=%async_computation.11 | async-start | bytes 5898240 | tf_op jit(solution)/shard_map/reduce_scatter | solution.py:463
  623.6 98.2 %copy-start.38 = (bf16[768,768]{1,0:T(8,128)(2,1)S(1)}, bf16[768,768]{1,0:T(8,128)(2,1)}, u32[]{:S(2)}) copy-start(bf16[768,768]{1,0:T(8,128)(2,1)} %param.21) | copy-start | bytes 3538948
  623.6 98.2 %copy-start.41 = (bf16[768,768]{1,0:T(8,128)(2,1)S(1)}, bf16[768,768]{1,0:T(8,128)(2,1)}, u32[]{:S(2)}) copy-start(bf16[768,768]{1,0:T(8,128)(2,1)} %param.19) | copy-start | bytes 3538948
  (47 other events, 151.3 us)
Sparse Core Ops, SparseCore 0:
  9.6 40.1 all-gather.2
  73.1 38.9 all-gather.4
  446.7 129.7 all-reduce.2
  581.9 139.8 all-reduce.4
  724.2 47.4 reduce-scatter.2
  774.1 47.9 reduce-scatter.4
